TPU v7x, 128 devices: a whole 4x4x4 slice. The times are simulated.
128 devices in a mesh: gx: 16 (over x_lo, z, core), gy: 8 (over y, x_hi).
Axes of the slice: x: 4 (x_hi: 2, x_lo: 2; x = x_hi * 2 + x_lo), y: 4, z: 4, core: 2. Of those that a mesh axis runs over, the one named last changes fastest.
Arguments:
- right_side: float32 [256, 256, 128], P('gx', 'gy'), may hold values from -6 to 6
- shift: float32 [256, 256, 128], P('gx', 'gy'), may hold values from 0.5 to 8
Outputs:
- solution_field: float32 [256, 256, 128], P('gx', 'gy')
- residual: float32 [256, 256, 128], P('gx', 'gy')
All inputs are finite; a program needn't handle non-finite values.
Results may differ from a plain program's by a relative error of at most 0.0003.
Values sent between devices are 32-bit elements; how exact they have to be, the bound alone decides.
No kernel may reach another device: no remote copies, remote signals or barrier semaphores. Data moves between devices by JAX's collectives and lax.ppermute only.
A program may use at most 128 MiB of HBM per device.

v0:
```python
import jax
import jax.numpy as jnp
from jax import lax
from jax.sharding import Mesh
from jax.sharding import PartitionSpec as P

ITERS = 3
LEVELS = 3
SWEEPS = 2
BOTTOM = 4
GX = ("gx_0", "gx_1", "gx_2")
GY = ("gy_0", "gy_1")
GX_GY = ("gx_0", "gx_1", "gx_2", "gy_0", "gy_1")
relaxation = 0.7
center_weight = 26.0


def with_halo(block, sides, width):
    for axis, dim in sides:
        count = lax.axis_size(axis)
        forward = [(i, i + 1) for i in range(count - 1)]
        backward = [(target, source) for source, target in forward]
        low = lax.ppermute(
            lax.slice_in_dim(block, block.shape[dim] - width, None, axis=dim), axis, forward
        )
        high = lax.ppermute(lax.slice_in_dim(block, 0, width, axis=dim), axis, backward)
        block = jnp.concatenate([low, block, high], axis=dim)
    return block


def one_axis_at_a_time(x, axes):
    for axis in axes:
        x = lax.psum(x, axis)
    return x


def neighbours(padded):
    total = padded[:, :, :-2] + padded[:, :, 1:-1] + padded[:, :, 2:]
    total = total[:, :-2] + total[:, 1:-1] + total[:, 2:]
    total = total[:-2] + total[1:-1] + total[2:]
    return total - padded[1:-1, 1:-1, 1:-1]


def coarsen(field):
    first, second, third = field.shape
    return field.reshape(first // 2, 2, second // 2, 2, third // 2, 2).mean(axis=(1, 3, 5))


def prolong(field):
    return jnp.repeat(jnp.repeat(jnp.repeat(field, 2, 0), 2, 1), 2, 2)


def level_diagonals(box_shift):
    result = []
    current = box_shift
    for level in range(LEVELS):
        result.append(center_weight + 4.0**level * current)
        if level + 1 < LEVELS:
            current = coarsen(current)
    return result


def sweep(guess, source, diag):
    return guess + relaxation * (source - (diag * guess - neighbours(jnp.pad(guess, 1)))) / diag


def vcycle(rhs, diags, level):
    diag = diags[level]
    source = 4.0**level * rhs
    count = BOTTOM if level == LEVELS - 1 else SWEEPS
    guess = relaxation * source / diag
    for turn in range(count - 1):
        guess = sweep(guess, source, diag)
    if level < LEVELS - 1:
        leftover = (source - (diag * guess - neighbours(jnp.pad(guess, 1)))) / 4.0**level
        guess = guess + prolong(vcycle(coarsen(leftover), diags, level + 1))
        for turn in range(SWEEPS):
            guess = sweep(guess, source, diag)
    return guess


def fold_band(padded, dim, width):
    length = padded.shape[dim]
    core = lax.slice_in_dim(padded, 2 * width, length - 2 * width, axis=dim)
    inner = core.shape[dim]
    lower = lax.slice_in_dim(padded, 0, width, axis=dim)
    upper = lax.slice_in_dim(padded, length - width, length, axis=dim)
    head = lax.slice_in_dim(core, 0, width, axis=dim) + lower
    middle = lax.slice_in_dim(core, width, inner - width, axis=dim)
    tail = lax.slice_in_dim(core, inner - width, inner, axis=dim) + upper
    return jnp.concatenate([head, middle, tail], axis=dim)


def on_device(right_side, shift):
    cells_x = right_side.shape[0]
    cells_y = right_side.shape[1]
    total_x = cells_x * lax.axis_size(GX)
    total_y = cells_y * lax.axis_size(GY)

    def extend(field):
        return with_halo(field, ((GX, 0), (GY, 1)), 2)

    shift_box = extend(shift)
    diags = level_diagonals(shift_box)
    rows = lax.axis_index(GX) * cells_x - 2 + jnp.arange(cells_x + 4, dtype=jnp.int32)
    cols = lax.axis_index(GY) * cells_y - 2 + jnp.arange(cells_y + 4, dtype=jnp.int32)
    row_ok = ((rows >= 0) & (rows < total_x)).astype(jnp.float32)
    col_ok = ((cols >= 0) & (cols < total_y)).astype(jnp.float32)
    grid_mask = row_ok[:, None, None] * col_ok[None, :, None]
    widths = ((1, 1), (1, 1), (0, 0))
    shift_grown = jnp.pad(shift_box, widths)

    def precondition_image(residual):
        local = vcycle(extend(residual), diags, 0) * grid_mask
        grown = jnp.pad(local, widths)
        image_local = (center_weight + shift_grown) * grown - neighbours(jnp.pad(grown, 1))
        stacked = jnp.stack([grown, image_local])
        returned = with_halo(stacked, ((GX, 1), (GY, 2)), 3)
        folded = fold_band(fold_band(returned, 1, 3), 2, 3)
        return (folded[0], folded[1])

    solution_field = jnp.zeros_like(right_side)
    residual = right_side

    def paired_sums(residual, precond, image):
        return (
            one_axis_at_a_time(jnp.sum(residual * precond), GX_GY),
            one_axis_at_a_time(jnp.sum(image * precond), GX_GY),
        )

    precond, image = precondition_image(residual)
    rz_now, product = paired_sums(residual, precond, image)
    alpha = rz_now / product
    direction, along = (precond, image)
    for step in range(ITERS):
        solution_field = solution_field + alpha * direction
        residual = residual - alpha * along
        if step + 1 < ITERS:
            precond, image = precondition_image(residual)
            rz_next, product = paired_sums(residual, precond, image)
            ratio = rz_next / rz_now
            alpha = rz_next / (product - ratio * rz_next / alpha)
            direction = precond + ratio * direction
            along = image + ratio * along
            rz_now = rz_next
    return (solution_field, residual)


def solution(mesh):
    split = Mesh(mesh.devices.reshape(2, 4, 2, 4, 2), ("gx_0", "gx_1", "gx_2", "gy_0", "gy_1"))
    in_specs = (P(GX, GY, None), P(GX, GY, None))
    out_specs = (P(GX, GY, None), P(GX, GY, None))
    return jax.shard_map(
        on_device, mesh=split, in_specs=in_specs, out_specs=out_specs, check_vma=False
    )
```

profile of v0, /device:TPU:42, one launch (start us, length us, event | category | flops | bytes accessed | tf_op | source)
XLA Modules:
  0.0 480.6 jit_solution(9280216936747103945)
XLA Ops:
  16.2 4.3 collective-permute-start.2
  28.0 4.8 %collective-permute-start.7 = (f32[20,2,128]{2,1,0:T(2,128)S(1)}, f32[20,2,128]{2,1,0:T(2,128)S(1)}, u32[]{:S(2)}, u32[]{:S(2)}) collective-permute-start(f32[20,2,128]{2,1,0:T(2,128)S(1)} %get-tuple-element.75), channel_id=1, source_target_pairs={{1,0},{2,1},{3,2},{4,3},{5,4},{6,5},{7,6},{9,8},{10,9},{11,10},{12... | collective-permute-start | bytes 61448 | tf_op jit(solution)/shard_map/ppermute | solution.py:26
  37.0 25.3 %reshape.131 = f32[10,2,18,2,64,2]{5,4,3,2,1,0:T(8,128)} reshape(f32[20,36,128]{2,1,0:T(8,128)S(1)} %fusion.95) | data formatting | bytes 737280 | tf_op jit(solution)/shard_map/reshape | solution.py:46
  62.3 25.2 %reshape.132 = f32[10,2,18,2,64,2]{5,4,3,2,1,0:T(8,128)} reshape(f32[20,36,128]{2,1,0:T(8,128)S(1)} %get-tuple-element.68) | data formatting | bytes 737280 | tf_op jit(solution)/shard_map/reshape | solution.py:46
  87.5 9.1 %reduce_sum.126 = f32[10,18,64]{2,1,0:T(8,128)S(1)} reduce(f32[10,2,18,2,64,2]{5,4,3,2,1,0:T(8,128)} %reshape.131, f32[]{:T(128)} %constant.67.clone.1), dimensions={1,3,5}, to_apply=%region_0.0 | reduce | flops 80640 | bytes 414724 | tf_op jit(solution)/shard_map/reduce_sum | solution.py:46
  96.6 9.1 %reduce_sum.127 = f32[10,18,64]{2,1,0:T(8,128)S(1)} reduce(f32[10,2,18,2,64,2]{5,4,3,2,1,0:T(8,128)} %reshape.132, f32[]{:T(128)} %constant.67.clone.1), dimensions={1,3,5}, to_apply=%region_1.0 | reduce | flops 80640 | bytes 414724 | tf_op jit(solution)/shard_map/reduce_sum | solution.py:46
  108.0 4.0 reshape.133
  112.3 4.2 div.159
  133.1 5.8 %collective-permute-start.10 = (f32[2,28,3,128]{3,0,2,1:T(2,128)S(1)}, f32[2,28,3,128]{3,0,2,1:T(2,128)S(1)}, u32[]{:S(2)}, u32[]{:S(2)}) collective-permute-start(f32[2,28,3,128]{3,0,2,1:T(2,128)S(1)} %get-tuple-element.48), channel_id=1, source_target_pairs={{0,1},{1,2},{2,3},{3,4},{4,5},{5,6},{6,7},{8,9},{9,10},{10,11},{11... | collective-permute-start | bytes 258056 | tf_op jit(solution)/shard_map/ppermute | solution.py:23
  142.1 4.9 %collective-permute-done.11 = f32[2,28,3,128]{3,0,2,1:T(2,128)S(1)} collective-permute-done((f32[2,28,3,128]{3,0,2,1:T(2,128)S(1)}, f32[2,28,3,128]{3,0,2,1:T(2,128)S(1)}, u32[]{:S(2)}, u32[]{:S(2)}) %collective-permute-start.11) | collective-permute-done | bytes 86048 | tf_op jit(solution)/shard_map/ppermute | solution.py:26
  151.3 5.6 %all-reduce.54 = (f32[]{:T(128)}, f32[]{:T(128)}) all-reduce(f32[]{:T(128)} %get-tuple-element.11, f32[]{:T(128)} %get-tuple-element.10), channel_id=1, replica_groups=mesh['gx_0'=2,'gx_1'=4,'gx_2'=2,'gy_0'=4,'gy_1'=2] {'gx_0'}, use_global_device_ids=true, to_apply=%region_5.6 | all-reduce | flops 2 | bytes 16 | tf_op jit(solution)/shard_map/psum | solution.py:33
  156.8 18.0 %all-reduce.45 = (f32[]{:T(128)}, f32[]{:T(128)}) all-reduce(f32[]{:T(128)} %get-tuple-element.40, f32[]{:T(128)} %get-tuple-element.41), channel_id=1, replica_groups=mesh['gx_0'=2,'gx_1'=4,'gx_2'=2,'gy_0'=4,'gy_1'=2] {'gx_1'}, use_global_device_ids=true, to_apply=%region_6.7 | all-reduce | flops 2 | bytes 16 | tf_op jit(solution)/shard_map/psum | solution.py:33
  177.9 9.0 %all-reduce.42 = (f32[]{:T(128)}, f32[]{:T(128)}) all-reduce(f32[]{:T(128)} %get-tuple-element.34, f32[]{:T(128)} %get-tuple-element.35), channel_id=1, replica_groups=mesh['gx_0'=2,'gx_1'=4,'gx_2'=2,'gy_0'=4,'gy_1'=2] {'gy_0'}, use_global_device_ids=true, to_apply=%region_8.9 | all-reduce | flops 2 | bytes 16 | tf_op jit(solution)/shard_map/psum | solution.py:33
  186.9 7.1 %all-reduce.48 = (f32[]{:T(128)}, f32[]{:T(128)}) all-reduce(f32[]{:T(128)} %get-tuple-element.16, f32[]{:T(128)} %get-tuple-element.17), channel_id=1, replica_groups=mesh['gx_0'=2,'gx_1'=4,'gx_2'=2,'gy_0'=4,'gy_1'=2] {'gy_1'}, use_global_device_ids=true, to_apply=%region_9.10 | all-reduce | flops 2 | bytes 16 | tf_op jit(solution)/shard_map/psum | solution.py:33
  205.7 5.0 %collective-permute-start.15 = (f32[20,2,128]{2,1,0:T(2,128)S(1)}, f32[20,2,128]{2,1,0:T(2,128)S(1)}, u32[]{:S(2)}, u32[]{:S(2)}) collective-permute-start(f32[20,2,128]{2,1,0:T(2,128)S(1)} %get-tuple-element.73), channel_id=1, source_target_pairs={{1,0},{2,1},{3,2},{4,3},{5,4},{6,5},{7,6},{9,8},{10,9},{11,10},{12... | collective-permute-start | bytes 61448 | tf_op jit(solution)/shard_map/ppermute | solution.py:26
  214.3 25.5 %reshape.140 = f32[10,2,18,2,64,2]{5,4,3,2,1,0:T(8,128)} reshape(f32[20,36,128]{2,1,0:T(8,128)S(1)} %fusion.74) | data formatting | bytes 737280 | tf_op jit(solution)/shard_map/reshape | solution.py:46
  239.7 9.1 %reduce_sum.132 = f32[10,18,64]{2,1,0:T(8,128)S(1)} reduce(f32[10,2,18,2,64,2]{5,4,3,2,1,0:T(8,128)} %reshape.140, f32[]{:T(128)} %constant.67.clone.1), dimensions={1,3,5}, to_apply=%region_16.17 | reduce | flops 80640 | bytes 414724 | tf_op jit(solution)/shard_map/reduce_sum | solution.py:46
  249.4 4.7 reshape.141
  273.6 4.6 collective-permute-start.18
  290.0 5.6 %all-reduce.53 = (f32[]{:T(128)}, f32[]{:T(128)}) all-reduce(f32[]{:T(128)} %get-tuple-element.9, f32[]{:T(128)} %get-tuple-element.8), channel_id=1, replica_groups=mesh['gx_0'=2,'gx_1'=4,'gx_2'=2,'gy_0'=4,'gy_1'=2] {'gx_0'}, use_global_device_ids=true, to_apply=%region_19.20 | all-reduce | flops 2 | bytes 16 | tf_op jit(solution)/shard_map/psum | solution.py:33
  295.6 12.6 %all-reduce.44 = (f32[]{:T(128)}, f32[]{:T(128)}) all-reduce(f32[]{:T(128)} %get-tuple-element.38, f32[]{:T(128)} %get-tuple-element.39), channel_id=1, replica_groups=mesh['gx_0'=2,'gx_1'=4,'gx_2'=2,'gy_0'=4,'gy_1'=2] {'gx_1'}, use_global_device_ids=true, to_apply=%region_20.21 | all-reduce | flops 2 | bytes 16 | tf_op jit(solution)/shard_map/psum | solution.py:33
  311.2 10.2 %all-reduce.41 = (f32[]{:T(128)}, f32[]{:T(128)}) all-reduce(f32[]{:T(128)} %get-tuple-element.32, f32[]{:T(128)} %get-tuple-element.33), channel_id=1, replica_groups=mesh['gx_0'=2,'gx_1'=4,'gx_2'=2,'gy_0'=4,'gy_1'=2] {'gy_0'}, use_global_device_ids=true, to_apply=%region_22.23 | all-reduce | flops 2 | bytes 16 | tf_op jit(solution)/shard_map/psum | solution.py:33
  321.4 7.0 %all-reduce.47 = (f32[]{:T(128)}, f32[]{:T(128)}) all-reduce(f32[]{:T(128)} %get-tuple-element.14, f32[]{:T(128)} %get-tuple-element.15), channel_id=1, replica_groups=mesh['gx_0'=2,'gx_1'=4,'gx_2'=2,'gy_0'=4,'gy_1'=2] {'gy_1'}, use_global_device_ids=true, to_apply=%region_23.24 | all-reduce | flops 2 | bytes 16 | tf_op jit(solution)/shard_map/psum | solution.py:33
  343.5 5.0 %collective-permute-start.23 = (f32[20,2,128]{2,1,0:T(2,128)S(1)}, f32[20,2,128]{2,1,0:T(2,128)S(1)}, u32[]{:S(2)}, u32[]{:S(2)}) collective-permute-start(f32[20,2,128]{2,1,0:T(2,128)S(1)} %get-tuple-element.71), channel_id=1, source_target_pairs={{1,0},{2,1},{3,2},{4,3},{5,4},{6,5},{7,6},{9,8},{10,9},{11,10},{12... | collective-permute-start | bytes 61448 | tf_op jit(solution)/shard_map/ppermute | solution.py:26
  352.8 26.0 %reshape.148 = f32[10,2,18,2,64,2]{5,4,3,2,1,0:T(8,128)} reshape(f32[20,36,128]{2,1,0:T(8,128)} %fusion.53) | data formatting | bytes 737280 | tf_op jit(solution)/shard_map/reshape | solution.py:46
  378.8 9.1 %reduce_sum.136 = f32[10,18,64]{2,1,0:T(8,128)S(1)} reduce(f32[10,2,18,2,64,2]{5,4,3,2,1,0:T(8,128)} %reshape.148, f32[]{:T(128)} %constant.67.clone.1), dimensions={1,3,5}, to_apply=%region_30.31 | reduce | flops 80640 | bytes 414724 | tf_op jit(solution)/shard_map/reduce_sum | solution.py:46
  388.5 4.7 reshape.149
  424.4 4.7 collective-permute-start.27
  436.0 5.6 %all-reduce.52 = (f32[]{:T(128)}, f32[]{:T(128)}) all-reduce(f32[]{:T(128)} %get-tuple-element.7, f32[]{:T(128)} %get-tuple-element.6), channel_id=1, replica_groups=mesh['gx_0'=2,'gx_1'=4,'gx_2'=2,'gy_0'=4,'gy_1'=2] {'gx_0'}, use_global_device_ids=true, to_apply=%region_33.34 | all-reduce | flops 2 | bytes 16 | tf_op jit(solution)/shard_map/psum | solution.py:33
  441.6 12.6 %all-reduce.43 = (f32[]{:T(128)}, f32[]{:T(128)}) all-reduce(f32[]{:T(128)} %get-tuple-element.36, f32[]{:T(128)} %get-tuple-element.37), channel_id=1, replica_groups=mesh['gx_0'=2,'gx_1'=4,'gx_2'=2,'gy_0'=4,'gy_1'=2] {'gx_1'}, use_global_device_ids=true, to_apply=%region_34.35 | all-reduce | flops 2 | bytes 16 | tf_op jit(solution)/shard_map/psum | solution.py:33
  457.3 11.2 %all-reduce.40 = (f32[]{:T(128)}, f32[]{:T(128)}) all-reduce(f32[]{:T(128)} %get-tuple-element.30, f32[]{:T(128)} %get-tuple-element.31), channel_id=1, replica_groups=mesh['gx_0'=2,'gx_1'=4,'gx_2'=2,'gy_0'=4,'gy_1'=2] {'gy_0'}, use_global_device_ids=true, to_apply=%region_36.37 | all-reduce | flops 2 | bytes 16 | tf_op jit(solution)/shard_map/psum | solution.py:33
  468.5 7.1 %all-reduce.46 = (f32[]{:T(128)}, f32[]{:T(128)}) all-reduce(f32[]{:T(128)} %get-tuple-element.12, f32[]{:T(128)} %get-tuple-element.13), channel_id=1, replica_groups=mesh['gx_0'=2,'gx_1'=4,'gx_2'=2,'gy_0'=4,'gy_1'=2] {'gy_1'}, use_global_device_ids=true, to_apply=%region_37.38 | all-reduce | flops 2 | bytes 16 | tf_op jit(solution)/shard_map/psum | solution.py:33
  (336 shorter events, 161.8 us)
Async XLA Ops:
  0.6 23.9 %copy-start.17 = (f32[16,32,128]{2,1,0:T(8,128)S(1)}, f32[16,32,128]{2,1,0:T(8,128)}, u32[]{:S(2)}) copy-start(f32[16,32,128]{2,1,0:T(8,128)} %param.3) | copy-start | bytes 786436
  1.5 23.1 %collective-permute-start.5 = (f32[2,32,128]{2,1,0:T(8,128)S(1)}, f32[2,32,128]{2,1,0:T(8,128)S(1)}, u32[]{:S(2)}, u32[]{:S(2)}) collective-permute-start(f32[2,32,128]{2,1,0:T(8,128)S(1)} %get-tuple-element.82), channel_id=1, source_target_pairs={{8,0},{16,8},{24,16},{32,24},{40,32},{48,40},{56,48},{64,56},{72,6... | collective-permute-start | bytes 98312 | tf_op jit(solution)/shard_map/ppermute | solution.py:26
  3.4 21.1 %collective-permute-start.4 = (f32[2,32,128]{2,1,0:T(8,128)S(1)}, f32[2,32,128]{2,1,0:T(8,128)S(1)}, u32[]{:S(2)}, u32[]{:S(2)}) collective-permute-start(f32[2,32,128]{2,1,0:T(8,128)S(1)} %get-tuple-element.83), channel_id=1, source_target_pairs={{0,8},{8,16},{16,24},{24,32},{32,40},{40,48},{48,56},{56,64},{64,7... | collective-permute-start | bytes 98312 | tf_op jit(solution)/shard_map/ppermute | solution.py:23
  6.6 9.6 %collective-permute-start.1 = (f32[2,32,128]{2,1,0:T(8,128)S(1)}, f32[2,32,128]{2,1,0:T(8,128)S(1)}, u32[]{:S(2)}, u32[]{:S(2)}) collective-permute-start(f32[2,32,128]{2,1,0:T(8,128)S(1)} %get-tuple-element.84), channel_id=1, source_target_pairs={{8,0},{16,8},{24,16},{32,24},{40,32},{48,40},{56,48},{64,56},{72,6... | collective-permute-start | bytes 98312 | tf_op jit(solution)/shard_map/ppermute | solution.py:26
  9.7 5.4 %collective-permute-start = (f32[2,32,128]{2,1,0:T(8,128)S(1)}, f32[2,32,128]{2,1,0:T(8,128)S(1)}, u32[]{:S(2)}, u32[]{:S(2)}) collective-permute-start(f32[2,32,128]{2,1,0:T(8,128)S(1)} %get-tuple-element.85), channel_id=1, source_target_pairs={{0,8},{8,16},{16,24},{24,32},{32,40},{40,48},{48,56},{56,64},{64,7... | collective-permute-start | bytes 98312 | tf_op jit(solution)/shard_map/ppermute | solution.py:23
  16.2 20.2 %copy-start.2 = (f32[20,32,128]{2,1,0:T(8,128)}, f32[20,32,128]{2,1,0:T(8,128)S(1)}, u32[]{:S(2)}) copy-start(f32[20,32,128]{2,1,0:T(8,128)S(1)} %constant_dynamic-update-slice_fusion) | copy-start | bytes 983044
  16.2 16.7 %collective-permute-start.2 = (f32[20,2,128]{2,1,0:T(2,128)S(1)}, f32[20,2,128]{2,1,0:T(2,128)S(1)}, u32[]{:S(2)}, u32[]{:S(2)}) collective-permute-start(f32[20,2,128]{2,1,0:T(2,128)S(1)} %get-tuple-element.76), channel_id=1, source_target_pairs={{0,1},{1,2},{2,3},{3,4},{4,5},{5,6},{6,7},{8,9},{9,10},{10,11},{11... | collective-permute-start | bytes 61448 | tf_op jit(solution)/shard_map/ppermute | solution.py:23
  20.5 12.4 %collective-permute-start.3 = (f32[20,2,128]{2,1,0:T(2,128)S(1)}, f32[20,2,128]{2,1,0:T(2,128)S(1)}, u32[]{:S(2)}, u32[]{:S(2)}) collective-permute-start(f32[20,2,128]{2,1,0:T(2,128)S(1)} %get-tuple-element.77), channel_id=1, source_target_pairs={{1,0},{2,1},{3,2},{4,3},{5,4},{6,5},{7,6},{9,8},{10,9},{11,10},{12... | collective-permute-start | bytes 61448 | tf_op jit(solution)/shard_map/ppermute | solution.py:26
  24.6 8.4 %collective-permute-start.6 = (f32[20,2,128]{2,1,0:T(2,128)S(1)}, f32[20,2,128]{2,1,0:T(2,128)S(1)}, u32[]{:S(2)}, u32[]{:S(2)}) collective-permute-start(f32[20,2,128]{2,1,0:T(2,128)S(1)} %get-tuple-element.74), channel_id=1, source_target_pairs={{0,1},{1,2},{2,3},{3,4},{4,5},{5,6},{6,7},{8,9},{9,10},{10,11},{11... | collective-permute-start | bytes 61448 | tf_op jit(solution)/shard_map/ppermute | solution.py:23
  28.0 7.2 %collective-permute-start.7 = (f32[20,2,128]{2,1,0:T(2,128)S(1)}, f32[20,2,128]{2,1,0:T(2,128)S(1)}, u32[]{:S(2)}, u32[]{:S(2)}) collective-permute-start(f32[20,2,128]{2,1,0:T(2,128)S(1)} %get-tuple-element.75), channel_id=1, source_target_pairs={{1,0},{2,1},{3,2},{4,3},{5,4},{6,5},{7,6},{9,8},{10,9},{11,10},{12... | collective-permute-start | bytes 61448 | tf_op jit(solution)/shard_map/ppermute | solution.py:26
  32.9 89.5 %copy-start.18 = (f32[20,36]{1,0:T(8,128)}, f32[20,36]{1,0:T(8,128)S(1)}, u32[]{:S(2)}) copy-start(f32[20,36]{1,0:T(8,128)S(1)} %broadcast_multiply_fusion.1) | copy-start | bytes 8644
  35.3 26.9 %copy-start = (f32[20,36,128]{2,1,0:T(8,128)}, f32[20,36,128]{2,1,0:T(8,128)S(1)}, u32[]{:S(2)}) copy-start(f32[20,36,128]{2,1,0:T(8,128)S(1)} %get-tuple-element.68) | copy-start | bytes 1105924
  125.0 6.1 %collective-permute-start.8 = (f32[2,3,38,128]{3,0,2,1:T(2,128)S(1)}, f32[2,3,38,128]{3,0,2,1:T(2,128)S(1)}, u32[]{:S(2)}, u32[]{:S(2)}) collective-permute-start(f32[2,3,38,128]{3,0,2,1:T(2,128)S(1)} %get-tuple-element.60), channel_id=1, source_target_pairs={{0,8},{8,16},{16,24},{24,32},{32,40},{40,48},{48,56},{56,64},{64,7... | collective-permute-start | bytes 350216 | tf_op jit(solution)/shard_map/ppermute | solution.py:23
  127.0 6.0 %collective-permute-start.9 = (f32[2,3,38,128]{3,0,2,1:T(2,128)S(1)}, f32[2,3,38,128]{3,0,2,1:T(2,128)S(1)}, u32[]{:S(2)}, u32[]{:S(2)}) collective-permute-start(f32[2,3,38,128]{3,0,2,1:T(2,128)S(1)} %get-tuple-element.61), channel_id=1, source_target_pairs={{8,0},{16,8},{24,16},{32,24},{40,32},{48,40},{56,48},{64,56},{72,6... | collective-permute-start | bytes 350216 | tf_op jit(solution)/shard_map/ppermute | solution.py:26
  133.1 9.0 %collective-permute-start.10 = (f32[2,28,3,128]{3,0,2,1:T(2,128)S(1)}, f32[2,28,3,128]{3,0,2,1:T(2,128)S(1)}, u32[]{:S(2)}, u32[]{:S(2)}) collective-permute-start(f32[2,28,3,128]{3,0,2,1:T(2,128)S(1)} %get-tuple-element.48), channel_id=1, source_target_pairs={{0,1},{1,2},{2,3},{3,4},{4,5},{5,6},{6,7},{8,9},{9,10},{10,11},{11... | collective-permute-start | bytes 258056 | tf_op jit(solution)/shard_map/ppermute | solution.py:23
  139.0 8.1 %collective-permute-start.11 = (f32[2,28,3,128]{3,0,2,1:T(2,128)S(1)}, f32[2,28,3,128]{3,0,2,1:T(2,128)S(1)}, u32[]{:S(2)}, u32[]{:S(2)}) collective-permute-start(f32[2,28,3,128]{3,0,2,1:T(2,128)S(1)} %get-tuple-element.49), channel_id=1, source_target_pairs={{1,0},{2,1},{3,2},{4,3},{5,4},{6,5},{7,6},{9,8},{10,9},{11,10},{12... | collective-permute-start | bytes 258056 | tf_op jit(solution)/shard_map/ppermute | solution.py:26
  195.2 5.6 %collective-permute-start.12 = (f32[2,32,128]{2,1,0:T(8,128)S(1)}, f32[2,32,128]{2,1,0:T(8,128)S(1)}, u32[]{:S(2)}, u32[]{:S(2)}) collective-permute-start(f32[2,32,128]{2,1,0:T(8,128)S(1)} %get-tuple-element.80), channel_id=1, source_target_pairs={{0,8},{8,16},{16,24},{24,32},{32,40},{40,48},{48,56},{56,64},{64,7... | collective-permute-start | bytes 98312 | tf_op jit(solution)/shard_map/ppermute | solution.py:23
  197.2 5.2 %collective-permute-start.13 = (f32[2,32,128]{2,1,0:T(8,128)S(1)}, f32[2,32,128]{2,1,0:T(8,128)S(1)}, u32[]{:S(2)}, u32[]{:S(2)}) collective-permute-start(f32[2,32,128]{2,1,0:T(8,128)S(1)} %get-tuple-element.81), channel_id=1, source_target_pairs={{8,0},{16,8},{24,16},{32,24},{40,32},{48,40},{56,48},{64,56},{72,6... | collective-permute-start | bytes 98312 | tf_op jit(solution)/shard_map/ppermute | solution.py:26
  202.4 8.3 %collective-permute-start.14 = (f32[20,2,128]{2,1,0:T(2,128)S(1)}, f32[20,2,128]{2,1,0:T(2,128)S(1)}, u32[]{:S(2)}, u32[]{:S(2)}) collective-permute-start(f32[20,2,128]{2,1,0:T(2,128)S(1)} %get-tuple-element.72), channel_id=1, source_target_pairs={{0,1},{1,2},{2,3},{3,4},{4,5},{5,6},{6,7},{8,9},{9,10},{10,11},{11... | collective-permute-start | bytes 61448 | tf_op jit(solution)/shard_map/ppermute | solution.py:23
  205.7 7.2 %collective-permute-start.15 = (f32[20,2,128]{2,1,0:T(2,128)S(1)}, f32[20,2,128]{2,1,0:T(2,128)S(1)}, u32[]{:S(2)}, u32[]{:S(2)}) collective-permute-start(f32[20,2,128]{2,1,0:T(2,128)S(1)} %get-tuple-element.73), channel_id=1, source_target_pairs={{1,0},{2,1},{3,2},{4,3},{5,4},{6,5},{7,6},{9,8},{10,9},{11,10},{12... | collective-permute-start | bytes 61448 | tf_op jit(solution)/shard_map/ppermute | solution.py:26
  265.5 6.1 %collective-permute-start.16 = (f32[2,3,38,128]{3,0,2,1:T(2,128)S(1)}, f32[2,3,38,128]{3,0,2,1:T(2,128)S(1)}, u32[]{:S(2)}, u32[]{:S(2)}) collective-permute-start(f32[2,3,38,128]{3,0,2,1:T(2,128)S(1)} %get-tuple-element.58), channel_id=1, source_target_pairs={{0,8},{8,16},{16,24},{24,32},{32,40},{40,48},{48,56},{56,64},{64,7... | collective-permute-start | bytes 350216 | tf_op jit(solution)/shard_map/ppermute | solution.py:23
  267.4 6.0 %collective-permute-start.17 = (f32[2,3,38,128]{3,0,2,1:T(2,128)S(1)}, f32[2,3,38,128]{3,0,2,1:T(2,128)S(1)}, u32[]{:S(2)}, u32[]{:S(2)}) collective-permute-start(f32[2,3,38,128]{3,0,2,1:T(2,128)S(1)} %get-tuple-element.59), channel_id=1, source_target_pairs={{8,0},{16,8},{24,16},{32,24},{40,32},{48,40},{56,48},{64,56},{72,6... | collective-permute-start | bytes 350216 | tf_op jit(solution)/shard_map/ppermute | solution.py:26
  273.6 8.8 %collective-permute-start.18 = (f32[2,28,3,128]{3,0,2,1:T(2,128)S(1)}, f32[2,28,3,128]{3,0,2,1:T(2,128)S(1)}, u32[]{:S(2)}, u32[]{:S(2)}) collective-permute-start(f32[2,28,3,128]{3,0,2,1:T(2,128)S(1)} %get-tuple-element.46), channel_id=1, source_target_pairs={{0,1},{1,2},{2,3},{3,4},{4,5},{5,6},{6,7},{8,9},{9,10},{10,11},{11... | collective-permute-start | bytes 258056 | tf_op jit(solution)/shard_map/ppermute | solution.py:23
  278.2 7.9 %collective-permute-start.19 = (f32[2,28,3,128]{3,0,2,1:T(2,128)S(1)}, f32[2,28,3,128]{3,0,2,1:T(2,128)S(1)}, u32[]{:S(2)}, u32[]{:S(2)}) collective-permute-start(f32[2,28,3,128]{3,0,2,1:T(2,128)S(1)} %get-tuple-element.47), channel_id=1, source_target_pairs={{1,0},{2,1},{3,2},{4,3},{5,4},{6,5},{7,6},{9,8},{10,9},{11,10},{12... | collective-permute-start | bytes 258056 | tf_op jit(solution)/shard_map/ppermute | solution.py:26
  333.0 5.6 %collective-permute-start.20 = (f32[2,32,128]{2,1,0:T(8,128)S(1)}, f32[2,32,128]{2,1,0:T(8,128)S(1)}, u32[]{:S(2)}, u32[]{:S(2)}) collective-permute-start(f32[2,32,128]{2,1,0:T(8,128)S(1)} %get-tuple-element.78), channel_id=1, source_target_pairs={{0,8},{8,16},{16,24},{24,32},{32,40},{40,48},{48,56},{56,64},{64,7... | collective-permute-start | bytes 98312 | tf_op jit(solution)/shard_map/ppermute | solution.py:23
  334.9 5.2 %collective-permute-start.21 = (f32[2,32,128]{2,1,0:T(8,128)S(1)}, f32[2,32,128]{2,1,0:T(8,128)S(1)}, u32[]{:S(2)}, u32[]{:S(2)}) collective-permute-start(f32[2,32,128]{2,1,0:T(8,128)S(1)} %get-tuple-element.79), channel_id=1, source_target_pairs={{8,0},{16,8},{24,16},{32,24},{40,32},{48,40},{56,48},{64,56},{72,6... | collective-permute-start | bytes 98312 | tf_op jit(solution)/shard_map/ppermute | solution.py:26
  340.2 8.3 %collective-permute-start.22 = (f32[20,2,128]{2,1,0:T(2,128)S(1)}, f32[20,2,128]{2,1,0:T(2,128)S(1)}, u32[]{:S(2)}, u32[]{:S(2)}) collective-permute-start(f32[20,2,128]{2,1,0:T(2,128)S(1)} %get-tuple-element.70), channel_id=1, source_target_pairs={{0,1},{1,2},{2,3},{3,4},{4,5},{5,6},{6,7},{8,9},{9,10},{10,11},{11... | collective-permute-start | bytes 61448 | tf_op jit(solution)/shard_map/ppermute | solution.py:23
  343.5 7.2 %collective-permute-start.23 = (f32[20,2,128]{2,1,0:T(2,128)S(1)}, f32[20,2,128]{2,1,0:T(2,128)S(1)}, u32[]{:S(2)}, u32[]{:S(2)}) collective-permute-start(f32[20,2,128]{2,1,0:T(2,128)S(1)} %get-tuple-element.71), channel_id=1, source_target_pairs={{1,0},{2,1},{3,2},{4,3},{5,4},{6,5},{7,6},{9,8},{10,9},{11,10},{12... | collective-permute-start | bytes 61448 | tf_op jit(solution)/shard_map/ppermute | solution.py:26
  412.7 6.1 %collective-permute-start.24 = (f32[2,3,38,128]{3,0,2,1:T(2,128)S(1)}, f32[2,3,38,128]{3,0,2,1:T(2,128)S(1)}, u32[]{:S(2)}, u32[]{:S(2)}) collective-permute-start(f32[2,3,38,128]{3,0,2,1:T(2,128)S(1)} %get-tuple-element.56), channel_id=1, source_target_pairs={{0,8},{8,16},{16,24},{24,32},{32,40},{40,48},{48,56},{56,64},{64,7... | collective-permute-start | bytes 350216 | tf_op jit(solution)/shard_map/ppermute | solution.py:23
  414.7 6.0 %collective-permute-start.25 = (f32[2,3,38,128]{3,0,2,1:T(2,128)S(1)}, f32[2,3,38,128]{3,0,2,1:T(2,128)S(1)}, u32[]{:S(2)}, u32[]{:S(2)}) collective-permute-start(f32[2,3,38,128]{3,0,2,1:T(2,128)S(1)} %get-tuple-element.57), channel_id=1, source_target_pairs={{8,0},{16,8},{24,16},{32,24},{40,32},{48,40},{56,48},{64,56},{72,6... | collective-permute-start | bytes 350216 | tf_op jit(solution)/shard_map/ppermute | solution.py:26
  420.8 8.8 %collective-permute-start.26 = (f32[2,28,3,128]{3,0,2,1:T(2,128)S(1)}, f32[2,28,3,128]{3,0,2,1:T(2,128)S(1)}, u32[]{:S(2)}, u32[]{:S(2)}) collective-permute-start(f32[2,28,3,128]{3,0,2,1:T(2,128)S(1)} %get-tuple-element.44), channel_id=1, source_target_pairs={{0,1},{1,2},{2,3},{3,4},{4,5},{5,6},{6,7},{8,9},{9,10},{10,11},{11... | collective-permute-start | bytes 258056 | tf_op jit(solution)/shard_map/ppermute | solution.py:23
  424.4 7.9 %collective-permute-start.27 = (f32[2,28,3,128]{3,0,2,1:T(2,128)S(1)}, f32[2,28,3,128]{3,0,2,1:T(2,128)S(1)}, u32[]{:S(2)}, u32[]{:S(2)}) collective-permute-start(f32[2,28,3,128]{3,0,2,1:T(2,128)S(1)} %get-tuple-element.45), channel_id=1, source_target_pairs={{1,0},{2,1},{3,2},{4,3},{5,4},{6,5},{7,6},{9,8},{10,9},{11,10},{12... | collective-permute-start | bytes 258056 | tf_op jit(solution)/shard_map/ppermute | solution.py:26
  (17 other events, 29.4 us)
where the time goes:
time: 490 us; the launch traced here: 481 us
  local copies, waits for them, and re-layouts  148 us (30%)
  blocking collectives  121 us (25%)
  starting transfers between devices  95.2 us (19%)
  other arithmetic  70.9 us (14%)
  waiting for transfers between devices  33.1 us (7%)
  between operations  12.3 us (3%)
    psum x15, blocking collectives, one_axis_at_a_time(): x = lax.psum(x, axis)  121 us
    reshape x7, local copies, waits for them, and re-layouts, coarsen(): field.reshape(first // 2, 2, second // 2, 2, third // 2, 2)  115 us
    ppermute x14, starting transfers between devices, with_halo(): lax.ppermute(lax.slice_in_dim(block, 0, width, axis=dim), axis, backward)  52.7 us
    ppermute x14, starting transfers between devices, with_halo(): lax.ppermute(lax.slice_in_dim(block, block.shape[dim] - width, None, axis...  42.5 us
    reduce_sum x8, other arithmetic, coarsen(): field.reshape(first // 2, 2, second // 2, 2, third // 2, 2)  41.2 us
    ppermute x14, waiting for transfers between devices, with_halo(): lax.ppermute(lax.slice_in_dim(block, 0, width, axis=dim), axis, backward)  26.4 us
    reshape x18, local copies, waits for them, and re-layouts, prolong(): return jnp.repeat(jnp.repeat(jnp.repeat(field, 2, 0), 2, 1), 2, 2)  10.5 us
  transfers between devices with their start and end apart: 28, of which 18 were waited for; matrix products, arithmetic and copies ran while one was open for 0% of the time, Pallas kernels for 0%

commit v1 on v0

--- a/solution.py
+++ b/solution.py
@@ -30,7 +30,8 @@
 
 def one_axis_at_a_time(x, axes):
     for axis in axes:
-        x = lax.psum(x, axis)
+        blocks = lax.all_gather(x, axis)
+        x = jnp.sum(blocks, axis=0)
     return x
 
 

time: 490 us -> 539 us (1.10)
  local copies, waits for them, and re-layouts: 148 us -> 194 us
  other arithmetic: 70.9 us -> 89.6 us
  blocking collectives: 121 us -> 108 us
    psum x15 -> x0, blocking collectives: 121 us -> none  [one_axis_at_a_time(): x = lax.psum(x, axis)]
    unnamed x0 -> x15, blocking collectives: none -> 108 us
    unnamed x46 -> x103, local copies, waits for them, and re-layouts: 5.49 us -> 49.6 us
    reduce_sum x0 -> x30, other arithmetic: none -> 19 us  [one_axis_at_a_time(): x = jnp.sum(blocks, axis=0)]
  transfers between devices with their start and end apart: 28 -> 28, of which waited for: 18 -> 16; matrix products, arithmetic and copies ran while one was open for 0% -> 0% of each run, Pallas kernels for 0% -> 0%
where the time goes in v1:
time: 539 us; the launch traced here: 530 us
  local copies, waits for them, and re-layouts  194 us (36%)
  blocking collectives  108 us (20%)
  starting transfers between devices  97.4 us (18%)
  other arithmetic  89.6 us (17%)
  waiting for transfers between devices  28.4 us (5%)
  between operations  12.3 us (2%)
    reshape x7, local copies, waits for them, and re-layouts, coarsen(): field.reshape(first // 2, 2, second // 2, 2, third // 2, 2)  114 us
    unnamed x15, blocking collectives  108 us
    ppermute x14, starting transfers between devices, with_halo(): lax.ppermute(lax.slice_in_dim(block, 0, width, axis=dim), axis, backward)  55.8 us
    unnamed x103, local copies, waits for them, and re-layouts  49.6 us
    reduce_sum x8, other arithmetic, coarsen(): field.reshape(first // 2, 2, second // 2, 2, third // 2, 2)  43 us
    ppermute x14, starting transfers between devices, with_halo(): lax.ppermute(lax.slice_in_dim(block, block.shape[dim] - width, None, axis...  41.7 us
    ppermute x14, waiting for transfers between devices, with_halo(): lax.ppermute(lax.slice_in_dim(block, 0, width, axis=dim), axis, backward)  26 us
    reduce_sum x30, other arithmetic, one_axis_at_a_time(): x = jnp.sum(blocks, axis=0)  19 us
  transfers between devices with their start and end apart: 28, of which 16 were waited for; matrix products, arithmetic and copies ran while one was open for 0% of the time, Pallas kernels for 0%

profile of v1, /device:TPU:42, one launch (start us, length us, event | category | flops | bytes accessed | tf_op | source)
XLA Modules:
  0.0 529.5 jit_solution(1044055314973434174)
XLA Ops:
  14.5 4.0 collective-permute-start.6
  18.5 4.2 collective-permute-start.7
  26.0 5.1 collective-permute-start.3
  35.0 25.3 %reshape.131 = f32[10,2,18,2,64,2]{5,4,3,2,1,0:T(8,128)} reshape(f32[20,36,128]{2,1,0:T(8,128)S(1)} %fusion.95) | data formatting | bytes 737280 | tf_op jit(solution)/shard_map/reshape | solution.py:47
  60.3 25.2 %reshape.132 = f32[10,2,18,2,64,2]{5,4,3,2,1,0:T(8,128)} reshape(f32[20,36,128]{2,1,0:T(8,128)S(1)} %get-tuple-element.68) | data formatting | bytes 737280 | tf_op jit(solution)/shard_map/reshape | solution.py:47
  85.5 9.1 %reduce_sum.396 = f32[10,18,64]{2,1,0:T(8,128)S(1)} reduce(f32[10,2,18,2,64,2]{5,4,3,2,1,0:T(8,128)} %reshape.131, f32[]{:T(128)} %constant.67.clone.1), dimensions={1,3,5}, to_apply=%region_0.0 | reduce | flops 80640 | bytes 414724 | tf_op jit(solution)/shard_map/reduce_sum | solution.py:47
  94.6 9.1 %reduce_sum.397 = f32[10,18,64]{2,1,0:T(8,128)S(1)} reduce(f32[10,2,18,2,64,2]{5,4,3,2,1,0:T(8,128)} %reshape.132, f32[]{:T(128)} %constant.67.clone.1), dimensions={1,3,5}, to_apply=%region_1.0 | reduce | flops 80640 | bytes 414724 | tf_op jit(solution)/shard_map/reduce_sum | solution.py:47
  110.0 5.1 div.159
  133.9 6.1 %collective-permute-start.10 = (f32[2,28,3,128]{3,0,2,1:T(2,128)S(1)}, f32[2,28,3,128]{3,0,2,1:T(2,128)S(1)}, u32[]{:S(2)}, u32[]{:S(2)}) collective-permute-start(f32[2,28,3,128]{3,0,2,1:T(2,128)S(1)} %get-tuple-element.48), channel_id=1, source_target_pairs={{0,1},{1,2},{2,3},{3,4},{4,5},{5,6},{6,7},{8,9},{9,10},{10,11},{11... | collective-permute-start | bytes 258056 | tf_op jit(solution)/shard_map/ppermute | solution.py:23
  142.8 5.2 collective-permute-done.11
  155.4 4.9 all-reduce.84
  165.1 14.6 %all-reduce.75 = (f32[4]{0:T(128)S(1)}, f32[4]{0:T(128)S(1)}) all-reduce(f32[4]{0:T(128)S(1)} %dynamic-update-slice.1, f32[4]{0:T(128)S(1)} %dynamic-update-slice.6), channel_id=1, replica_groups=mesh['gx_0'=2,'gx_1'=4,'gx_2'=2,'gy_0'=4,'gy_1'=2] {'gx_1'}, use_global_device_ids=true, to_apply=%add.41 | all-reduce | flops 8 | bytes 64
  191.7 8.4 %all-reduce.72 = (f32[4]{0:T(128)S(1)}, f32[4]{0:T(128)S(1)}) all-reduce(f32[4]{0:T(128)S(1)} %dynamic-update-slice.3, f32[4]{0:T(128)S(1)} %dynamic-update-slice.8), channel_id=1, replica_groups=mesh['gx_0'=2,'gx_1'=4,'gx_2'=2,'gy_0'=4,'gy_1'=2] {'gy_0'}, use_global_device_ids=true, to_apply=%add.43 | all-reduce | flops 8 | bytes 64
  204.1 6.4 %all-reduce.78 = (f32[2]{0:T(128)S(1)}, f32[2]{0:T(128)S(1)}) all-reduce(f32[2]{0:T(128)S(1)} %dynamic-update-slice.4, f32[2]{0:T(128)S(1)} %dynamic-update-slice.9), channel_id=1, replica_groups=mesh['gx_0'=2,'gx_1'=4,'gx_2'=2,'gy_0'=4,'gy_1'=2] {'gy_1'}, use_global_device_ids=true, to_apply=%add.44 | all-reduce | flops 4 | bytes 32
  223.4 5.5 %collective-permute-start.15 = (f32[20,2,128]{2,1,0:T(2,128)S(1)}, f32[20,2,128]{2,1,0:T(2,128)S(1)}, u32[]{:S(2)}, u32[]{:S(2)}) collective-permute-start(f32[20,2,128]{2,1,0:T(2,128)S(1)} %get-tuple-element.73), channel_id=1, source_target_pairs={{1,0},{2,1},{3,2},{4,3},{5,4},{6,5},{7,6},{9,8},{10,9},{11,10},{12... | collective-permute-start | bytes 61448 | tf_op jit(solution)/shard_map/ppermute | solution.py:26
  232.0 25.3 %reshape.140 = f32[10,2,18,2,64,2]{5,4,3,2,1,0:T(8,128)} reshape(f32[20,36,128]{2,1,0:T(8,128)S(1)} %fusion.74) | data formatting | bytes 737280 | tf_op jit(solution)/shard_map/reshape | solution.py:47
  257.3 9.1 %reduce_sum.412 = f32[10,18,64]{2,1,0:T(8,128)S(1)} reduce(f32[10,2,18,2,64,2]{5,4,3,2,1,0:T(8,128)} %reshape.140, f32[]{:T(128)} %constant.67.clone.1), dimensions={1,3,5}, to_apply=%region_16.17 | reduce | flops 80640 | bytes 414724 | tf_op jit(solution)/shard_map/reduce_sum | solution.py:47
  266.9 4.7 reshape.141
  293.9 4.7 collective-permute-start.18
  312.8 4.9 all-reduce.83
  321.9 11.9 %all-reduce.74 = (f32[4]{0:T(128)S(1)}, f32[4]{0:T(128)S(1)}) all-reduce(f32[4]{0:T(128)S(1)} %dynamic-update-slice.11, f32[4]{0:T(128)S(1)} %dynamic-update-slice.16), channel_id=1, replica_groups=mesh['gx_0'=2,'gx_1'=4,'gx_2'=2,'gy_0'=4,'gy_1'=2] {'gx_1'}, use_global_device_ids=true, to_apply=%add.51 | all-reduce | flops 8 | bytes 64
  344.9 9.6 %all-reduce.71 = (f32[4]{0:T(128)S(1)}, f32[4]{0:T(128)S(1)}) all-reduce(f32[4]{0:T(128)S(1)} %dynamic-update-slice.13, f32[4]{0:T(128)S(1)} %dynamic-update-slice.18), channel_id=1, replica_groups=mesh['gx_0'=2,'gx_1'=4,'gx_2'=2,'gy_0'=4,'gy_1'=2] {'gy_0'}, use_global_device_ids=true, to_apply=%add.53 | all-reduce | flops 8 | bytes 64
  358.6 6.4 %all-reduce.77 = (f32[2]{0:T(128)S(1)}, f32[2]{0:T(128)S(1)}) all-reduce(f32[2]{0:T(128)S(1)} %dynamic-update-slice.14, f32[2]{0:T(128)S(1)} %dynamic-update-slice.19), channel_id=1, replica_groups=mesh['gx_0'=2,'gx_1'=4,'gx_2'=2,'gy_0'=4,'gy_1'=2] {'gy_1'}, use_global_device_ids=true, to_apply=%add.54 | all-reduce | flops 4 | bytes 32
  381.0 5.1 collective-permute-start.23
  389.6 25.3 %reshape.148 = f32[10,2,18,2,64,2]{5,4,3,2,1,0:T(8,128)} reshape(f32[20,36,128]{2,1,0:T(8,128)S(1)} %fusion.53) | data formatting | bytes 737280 | tf_op jit(solution)/shard_map/reshape | solution.py:47
  414.8 9.1 %reduce_sum.426 = f32[10,18,64]{2,1,0:T(8,128)S(1)} reduce(f32[10,2,18,2,64,2]{5,4,3,2,1,0:T(8,128)} %reshape.148, f32[]{:T(128)} %constant.67.clone.1), dimensions={1,3,5}, to_apply=%region_30.31 | reduce | flops 80640 | bytes 414724 | tf_op jit(solution)/shard_map/reduce_sum | solution.py:47
  424.5 4.7 reshape.149
  456.9 4.7 collective-permute-start.27
  471.0 4.9 all-reduce.82
  479.9 11.9 %all-reduce.73 = (f32[4]{0:T(128)S(1)}, f32[4]{0:T(128)S(1)}) all-reduce(f32[4]{0:T(128)S(1)} %dynamic-update-slice.21, f32[4]{0:T(128)S(1)} %dynamic-update-slice.26), channel_id=1, replica_groups=mesh['gx_0'=2,'gx_1'=4,'gx_2'=2,'gy_0'=4,'gy_1'=2] {'gx_1'}, use_global_device_ids=true, to_apply=%add.61 | all-reduce | flops 8 | bytes 64
  502.4 10.6 %all-reduce.70 = (f32[4]{0:T(128)S(1)}, f32[4]{0:T(128)S(1)}) all-reduce(f32[4]{0:T(128)S(1)} %dynamic-update-slice.23, f32[4]{0:T(128)S(1)} %dynamic-update-slice.28), channel_id=1, replica_groups=mesh['gx_0'=2,'gx_1'=4,'gx_2'=2,'gy_0'=4,'gy_1'=2] {'gy_0'}, use_global_device_ids=true, to_apply=%add.63 | all-reduce | flops 8 | bytes 64
  516.9 6.4 %all-reduce.76 = (f32[2]{0:T(128)S(1)}, f32[2]{0:T(128)S(1)}) all-reduce(f32[2]{0:T(128)S(1)} %dynamic-update-slice.24, f32[2]{0:T(128)S(1)} %dynamic-update-slice.29), channel_id=1, replica_groups=mesh['gx_0'=2,'gx_1'=4,'gx_2'=2,'gy_0'=4,'gy_1'=2] {'gy_1'}, use_global_device_ids=true, to_apply=%add.64 | all-reduce | flops 4 | bytes 32
  (423 shorter events, 219.6 us)
Async XLA Ops:
  0.6 22.1 %copy-start.8 = (f32[16,32,128]{2,1,0:T(8,128)S(1)}, f32[16,32,128]{2,1,0:T(8,128)}, u32[]{:S(2)}) copy-start(f32[16,32,128]{2,1,0:T(8,128)} %param.2) | copy-start | bytes 786436
  1.5 12.0 %collective-permute-start.4 = (f32[2,32,128]{2,1,0:T(8,128)S(1)}, f32[2,32,128]{2,1,0:T(8,128)S(1)}, u32[]{:S(2)}, u32[]{:S(2)}) collective-permute-start(f32[2,32,128]{2,1,0:T(8,128)S(1)} %get-tuple-element.83), channel_id=1, source_target_pairs={{0,8},{8,16},{16,24},{24,32},{32,40},{40,48},{48,56},{56,64},{64,7... | collective-permute-start | bytes 98312 | tf_op jit(solution)/shard_map/ppermute | solution.py:23
  3.4 11.0 %collective-permute-start.5 = (f32[2,32,128]{2,1,0:T(8,128)S(1)}, f32[2,32,128]{2,1,0:T(8,128)S(1)}, u32[]{:S(2)}, u32[]{:S(2)}) collective-permute-start(f32[2,32,128]{2,1,0:T(8,128)S(1)} %get-tuple-element.82), channel_id=1, source_target_pairs={{8,0},{16,8},{24,16},{32,24},{40,32},{48,40},{56,48},{64,56},{72,6... | collective-permute-start | bytes 98312 | tf_op jit(solution)/shard_map/ppermute | solution.py:26
  7.8 14.9 %collective-permute-start = (f32[2,32,128]{2,1,0:T(8,128)S(1)}, f32[2,32,128]{2,1,0:T(8,128)S(1)}, u32[]{:S(2)}, u32[]{:S(2)}) collective-permute-start(f32[2,32,128]{2,1,0:T(8,128)S(1)} %get-tuple-element.85), channel_id=1, source_target_pairs={{0,8},{8,16},{16,24},{24,32},{32,40},{40,48},{48,56},{56,64},{64,7... | collective-permute-start | bytes 98312 | tf_op jit(solution)/shard_map/ppermute | solution.py:23
  10.0 12.8 %collective-permute-start.1 = (f32[2,32,128]{2,1,0:T(8,128)S(1)}, f32[2,32,128]{2,1,0:T(8,128)S(1)}, u32[]{:S(2)}, u32[]{:S(2)}) collective-permute-start(f32[2,32,128]{2,1,0:T(8,128)S(1)} %get-tuple-element.84), channel_id=1, source_target_pairs={{8,0},{16,8},{24,16},{32,24},{40,32},{48,40},{56,48},{64,56},{72,6... | collective-permute-start | bytes 98312 | tf_op jit(solution)/shard_map/ppermute | solution.py:26
  14.5 16.7 %collective-permute-start.6 = (f32[20,2,128]{2,1,0:T(2,128)S(1)}, f32[20,2,128]{2,1,0:T(2,128)S(1)}, u32[]{:S(2)}, u32[]{:S(2)}) collective-permute-start(f32[20,2,128]{2,1,0:T(2,128)S(1)} %get-tuple-element.74), channel_id=1, source_target_pairs={{0,1},{1,2},{2,3},{3,4},{4,5},{5,6},{6,7},{8,9},{9,10},{10,11},{11... | collective-permute-start | bytes 61448 | tf_op jit(solution)/shard_map/ppermute | solution.py:23
  18.5 12.7 %collective-permute-start.7 = (f32[20,2,128]{2,1,0:T(2,128)S(1)}, f32[20,2,128]{2,1,0:T(2,128)S(1)}, u32[]{:S(2)}, u32[]{:S(2)}) collective-permute-start(f32[20,2,128]{2,1,0:T(2,128)S(1)} %get-tuple-element.75), channel_id=1, source_target_pairs={{1,0},{2,1},{3,2},{4,3},{5,4},{6,5},{7,6},{9,8},{10,9},{11,10},{12... | collective-permute-start | bytes 61448 | tf_op jit(solution)/shard_map/ppermute | solution.py:26
  22.9 8.3 %collective-permute-start.2 = (f32[20,2,128]{2,1,0:T(2,128)S(1)}, f32[20,2,128]{2,1,0:T(2,128)S(1)}, u32[]{:S(2)}, u32[]{:S(2)}) collective-permute-start(f32[20,2,128]{2,1,0:T(2,128)S(1)} %get-tuple-element.76), channel_id=1, source_target_pairs={{0,1},{1,2},{2,3},{3,4},{4,5},{5,6},{6,7},{8,9},{9,10},{10,11},{11... | collective-permute-start | bytes 61448 | tf_op jit(solution)/shard_map/ppermute | solution.py:23
  26.0 7.2 %collective-permute-start.3 = (f32[20,2,128]{2,1,0:T(2,128)S(1)}, f32[20,2,128]{2,1,0:T(2,128)S(1)}, u32[]{:S(2)}, u32[]{:S(2)}) collective-permute-start(f32[20,2,128]{2,1,0:T(2,128)S(1)} %get-tuple-element.77), channel_id=1, source_target_pairs={{1,0},{2,1},{3,2},{4,3},{5,4},{6,5},{7,6},{9,8},{10,9},{11,10},{12... | collective-permute-start | bytes 61448 | tf_op jit(solution)/shard_map/ppermute | solution.py:26
  33.3 27.0 %copy-start = (f32[20,36,128]{2,1,0:T(8,128)}, f32[20,36,128]{2,1,0:T(8,128)S(1)}, u32[]{:S(2)}) copy-start(f32[20,36,128]{2,1,0:T(8,128)S(1)} %get-tuple-element.68) | copy-start | bytes 1105924
  125.8 6.1 %collective-permute-start.8 = (f32[2,3,38,128]{3,0,2,1:T(2,128)S(1)}, f32[2,3,38,128]{3,0,2,1:T(2,128)S(1)}, u32[]{:S(2)}, u32[]{:S(2)}) collective-permute-start(f32[2,3,38,128]{3,0,2,1:T(2,128)S(1)} %get-tuple-element.60), channel_id=1, source_target_pairs={{0,8},{8,16},{16,24},{24,32},{32,40},{40,48},{48,56},{56,64},{64,7... | collective-permute-start | bytes 350216 | tf_op jit(solution)/shard_map/ppermute | solution.py:23
  127.8 6.0 %collective-permute-start.9 = (f32[2,3,38,128]{3,0,2,1:T(2,128)S(1)}, f32[2,3,38,128]{3,0,2,1:T(2,128)S(1)}, u32[]{:S(2)}, u32[]{:S(2)}) collective-permute-start(f32[2,3,38,128]{3,0,2,1:T(2,128)S(1)} %get-tuple-element.61), channel_id=1, source_target_pairs={{8,0},{16,8},{24,16},{32,24},{40,32},{48,40},{56,48},{64,56},{72,6... | collective-permute-start | bytes 350216 | tf_op jit(solution)/shard_map/ppermute | solution.py:26
  133.9 8.9 %collective-permute-start.10 = (f32[2,28,3,128]{3,0,2,1:T(2,128)S(1)}, f32[2,28,3,128]{3,0,2,1:T(2,128)S(1)}, u32[]{:S(2)}, u32[]{:S(2)}) collective-permute-start(f32[2,28,3,128]{3,0,2,1:T(2,128)S(1)} %get-tuple-element.48), channel_id=1, source_target_pairs={{0,1},{1,2},{2,3},{3,4},{4,5},{5,6},{6,7},{8,9},{9,10},{10,11},{11... | collective-permute-start | bytes 258056 | tf_op jit(solution)/shard_map/ppermute | solution.py:23
  140.1 7.9 %collective-permute-start.11 = (f32[2,28,3,128]{3,0,2,1:T(2,128)S(1)}, f32[2,28,3,128]{3,0,2,1:T(2,128)S(1)}, u32[]{:S(2)}, u32[]{:S(2)}) collective-permute-start(f32[2,28,3,128]{3,0,2,1:T(2,128)S(1)} %get-tuple-element.49), channel_id=1, source_target_pairs={{1,0},{2,1},{3,2},{4,3},{5,4},{6,5},{7,6},{9,8},{10,9},{11,10},{12... | collective-permute-start | bytes 258056 | tf_op jit(solution)/shard_map/ppermute | solution.py:26
  150.7 33.2 %copy-start.13 = (u32[128]{0:T(128)S(1)}, u32[128]{0:T(128)}, u32[]{:S(2)}) copy-start(u32[128]{0:T(128)} %constant.182) | copy-start | bytes 1540
  150.7 40.3 %copy-start.12 = (u32[128]{0:T(128)S(1)}, u32[128]{0:T(128)}, u32[]{:S(2)}) copy-start(u32[128]{0:T(128)} %constant.187) | copy-start | bytes 1540
  213.1 5.6 %collective-permute-start.12 = (f32[2,32,128]{2,1,0:T(8,128)S(1)}, f32[2,32,128]{2,1,0:T(8,128)S(1)}, u32[]{:S(2)}, u32[]{:S(2)}) collective-permute-start(f32[2,32,128]{2,1,0:T(8,128)S(1)} %get-tuple-element.80), channel_id=1, source_target_pairs={{0,8},{8,16},{16,24},{24,32},{32,40},{40,48},{48,56},{56,64},{64,7... | collective-permute-start | bytes 98312 | tf_op jit(solution)/shard_map/ppermute | solution.py:23
  215.1 5.2 collective-permute-start.13
  220.3 8.7 %collective-permute-start.14 = (f32[20,2,128]{2,1,0:T(2,128)S(1)}, f32[20,2,128]{2,1,0:T(2,128)S(1)}, u32[]{:S(2)}, u32[]{:S(2)}) collective-permute-start(f32[20,2,128]{2,1,0:T(2,128)S(1)} %get-tuple-element.72), channel_id=1, source_target_pairs={{0,1},{1,2},{2,3},{3,4},{4,5},{5,6},{6,7},{8,9},{9,10},{10,11},{11... | collective-permute-start | bytes 61448 | tf_op jit(solution)/shard_map/ppermute | solution.py:23
  223.4 7.2 %collective-permute-start.15 = (f32[20,2,128]{2,1,0:T(2,128)S(1)}, f32[20,2,128]{2,1,0:T(2,128)S(1)}, u32[]{:S(2)}, u32[]{:S(2)}) collective-permute-start(f32[20,2,128]{2,1,0:T(2,128)S(1)} %get-tuple-element.73), channel_id=1, source_target_pairs={{1,0},{2,1},{3,2},{4,3},{5,4},{6,5},{7,6},{9,8},{10,9},{11,10},{12... | collective-permute-start | bytes 61448 | tf_op jit(solution)/shard_map/ppermute | solution.py:26
  285.8 6.1 %collective-permute-start.16 = (f32[2,3,38,128]{3,0,2,1:T(2,128)S(1)}, f32[2,3,38,128]{3,0,2,1:T(2,128)S(1)}, u32[]{:S(2)}, u32[]{:S(2)}) collective-permute-start(f32[2,3,38,128]{3,0,2,1:T(2,128)S(1)} %get-tuple-element.58), channel_id=1, source_target_pairs={{0,8},{8,16},{16,24},{24,32},{32,40},{40,48},{48,56},{56,64},{64,7... | collective-permute-start | bytes 350216 | tf_op jit(solution)/shard_map/ppermute | solution.py:23
  287.7 6.0 %collective-permute-start.17 = (f32[2,3,38,128]{3,0,2,1:T(2,128)S(1)}, f32[2,3,38,128]{3,0,2,1:T(2,128)S(1)}, u32[]{:S(2)}, u32[]{:S(2)}) collective-permute-start(f32[2,3,38,128]{3,0,2,1:T(2,128)S(1)} %get-tuple-element.59), channel_id=1, source_target_pairs={{8,0},{16,8},{24,16},{32,24},{40,32},{48,40},{56,48},{64,56},{72,6... | collective-permute-start | bytes 350216 | tf_op jit(solution)/shard_map/ppermute | solution.py:26
  293.9 8.8 %collective-permute-start.18 = (f32[2,28,3,128]{3,0,2,1:T(2,128)S(1)}, f32[2,28,3,128]{3,0,2,1:T(2,128)S(1)}, u32[]{:S(2)}, u32[]{:S(2)}) collective-permute-start(f32[2,28,3,128]{3,0,2,1:T(2,128)S(1)} %get-tuple-element.46), channel_id=1, source_target_pairs={{0,1},{1,2},{2,3},{3,4},{4,5},{5,6},{6,7},{8,9},{9,10},{10,11},{11... | collective-permute-start | bytes 258056 | tf_op jit(solution)/shard_map/ppermute | solution.py:23
  298.6 7.9 %collective-permute-start.19 = (f32[2,28,3,128]{3,0,2,1:T(2,128)S(1)}, f32[2,28,3,128]{3,0,2,1:T(2,128)S(1)}, u32[]{:S(2)}, u32[]{:S(2)}) collective-permute-start(f32[2,28,3,128]{3,0,2,1:T(2,128)S(1)} %get-tuple-element.47), channel_id=1, source_target_pairs={{1,0},{2,1},{3,2},{4,3},{5,4},{6,5},{7,6},{9,8},{10,9},{11,10},{12... | collective-permute-start | bytes 258056 | tf_op jit(solution)/shard_map/ppermute | solution.py:26
  370.7 5.6 %collective-permute-start.20 = (f32[2,32,128]{2,1,0:T(8,128)S(1)}, f32[2,32,128]{2,1,0:T(8,128)S(1)}, u32[]{:S(2)}, u32[]{:S(2)}) collective-permute-start(f32[2,32,128]{2,1,0:T(8,128)S(1)} %get-tuple-element.78), channel_id=1, source_target_pairs={{0,8},{8,16},{16,24},{24,32},{32,40},{40,48},{48,56},{56,64},{64,7... | collective-permute-start | bytes 98312 | tf_op jit(solution)/shard_map/ppermute | solution.py:23
  372.6 5.2 collective-permute-start.21
  377.9 8.3 %collective-permute-start.22 = (f32[20,2,128]{2,1,0:T(2,128)S(1)}, f32[20,2,128]{2,1,0:T(2,128)S(1)}, u32[]{:S(2)}, u32[]{:S(2)}) collective-permute-start(f32[20,2,128]{2,1,0:T(2,128)S(1)} %get-tuple-element.70), channel_id=1, source_target_pairs={{0,1},{1,2},{2,3},{3,4},{4,5},{5,6},{6,7},{8,9},{9,10},{10,11},{11... | collective-permute-start | bytes 61448 | tf_op jit(solution)/shard_map/ppermute | solution.py:23
  381.0 7.2 %collective-permute-start.23 = (f32[20,2,128]{2,1,0:T(2,128)S(1)}, f32[20,2,128]{2,1,0:T(2,128)S(1)}, u32[]{:S(2)}, u32[]{:S(2)}) collective-permute-start(f32[20,2,128]{2,1,0:T(2,128)S(1)} %get-tuple-element.71), channel_id=1, source_target_pairs={{1,0},{2,1},{3,2},{4,3},{5,4},{6,5},{7,6},{9,8},{10,9},{11,10},{12... | collective-permute-start | bytes 61448 | tf_op jit(solution)/shard_map/ppermute | solution.py:26
  445.1 6.1 %collective-permute-start.24 = (f32[2,3,38,128]{3,0,2,1:T(2,128)S(1)}, f32[2,3,38,128]{3,0,2,1:T(2,128)S(1)}, u32[]{:S(2)}, u32[]{:S(2)}) collective-permute-start(f32[2,3,38,128]{3,0,2,1:T(2,128)S(1)} %get-tuple-element.56), channel_id=1, source_target_pairs={{0,8},{8,16},{16,24},{24,32},{32,40},{40,48},{48,56},{56,64},{64,7... | collective-permute-start | bytes 350216 | tf_op jit(solution)/shard_map/ppermute | solution.py:23
  447.0 6.0 %collective-permute-start.25 = (f32[2,3,38,128]{3,0,2,1:T(2,128)S(1)}, f32[2,3,38,128]{3,0,2,1:T(2,128)S(1)}, u32[]{:S(2)}, u32[]{:S(2)}) collective-permute-start(f32[2,3,38,128]{3,0,2,1:T(2,128)S(1)} %get-tuple-element.57), channel_id=1, source_target_pairs={{8,0},{16,8},{24,16},{32,24},{40,32},{48,40},{56,48},{64,56},{72,6... | collective-permute-start | bytes 350216 | tf_op jit(solution)/shard_map/ppermute | solution.py:26
  453.2 8.8 %collective-permute-start.26 = (f32[2,28,3,128]{3,0,2,1:T(2,128)S(1)}, f32[2,28,3,128]{3,0,2,1:T(2,128)S(1)}, u32[]{:S(2)}, u32[]{:S(2)}) collective-permute-start(f32[2,28,3,128]{3,0,2,1:T(2,128)S(1)} %get-tuple-element.44), channel_id=1, source_target_pairs={{0,1},{1,2},{2,3},{3,4},{4,5},{5,6},{6,7},{8,9},{9,10},{10,11},{11... | collective-permute-start | bytes 258056 | tf_op jit(solution)/shard_map/ppermute | solution.py:23
  456.9 7.9 %collective-permute-start.27 = (f32[2,28,3,128]{3,0,2,1:T(2,128)S(1)}, f32[2,28,3,128]{3,0,2,1:T(2,128)S(1)}, u32[]{:S(2)}, u32[]{:S(2)}) collective-permute-start(f32[2,28,3,128]{3,0,2,1:T(2,128)S(1)} %get-tuple-element.45), channel_id=1, source_target_pairs={{1,0},{2,1},{3,2},{4,3},{5,4},{6,5},{7,6},{9,8},{10,9},{11,10},{12... | collective-permute-start | bytes 258056 | tf_op jit(solution)/shard_map/ppermute | solution.py:26
  (13 other events, 63.5 us)
